TPU v7x, 32 devices: a whole 2x2x4 slice. The times are simulated.
32 devices in a mesh: row: 4 (over y, x), col: 4 (over z), band: 2 (over core).
Axes of the slice: x: 2, y: 2, z: 4, core: 2. Of those that a mesh axis runs over, the one named last changes fastest.
Arguments:
- freq_index: int32 [2], replicated, may hold values from 0 to 32
- band_energy: float32 [8], replicated, may hold values from -4 to 4
- pole_amp: float32 [4096, 4096], P('row', 'col'), may hold values from -6 to 6
- pole_freq: float32 [4096, 4096], P('row', 'col'), may hold values from 0.5 to 4
- left_pieces: bfloat16 [8, 256, 4096], P(('col', 'band'), None, 'row'), may hold values from -0.055664062 to 0.055664062
- right_pieces: bfloat16 [8, 256, 4096], P(('row', 'band'), None, 'col'), may hold values from -0.055664062 to 0.055664062
Outputs:
- sigma: float32 [2, 256, 256], P(None, ('row', 'col', 'band'))
All inputs are finite; a program needn't handle non-finite values.
Results may differ from a plain program's by a relative error of at most 0.0055.
Values may be sent and summed in bfloat16 or wider, within the bound.
No kernel may reach another device: no remote copies, remote signals or barrier semaphores. Data moves between devices by JAX's collectives and lax.ppermute only.
A program may use at most 128 MiB of HBM per device.

v0:
```python
import jax
import jax.numpy as jnp
from jax import lax
from jax.sharding import PartitionSpec as P


def body(freq_index, band_energy, pole_amp, pole_freq, left_pieces, right_pieces):
    bpiece = left_pieces.shape[0]
    nstate = left_pieces.shape[1]
    nfreq = freq_index.shape[0]
    nband = lax.axis_size("band")
    group = lax.axis_index("band")
    freq = -4.0 + 0.25 * freq_index.astype(jnp.float32)
    right_all = lax.all_gather(right_pieces, "row", axis=0, tiled=True)

    def energy_at(position):
        overall = (position // bpiece * nband + group) * bpiece + position % bpiece
        return lax.dynamic_index_in_dim(band_energy, overall, 0, False)

    def add_band(total, left_band, position):
        right_band = lax.dynamic_index_in_dim(right_all, position, 0, False)
        energy = energy_at(position)
        results = []
        for w in range(nfreq):
            distance = freq[w] - energy - pole_freq
            screened = (pole_amp * distance / (distance * distance + 0.25)).astype(jnp.bfloat16)
            partial_value = jnp.dot(left_band, screened, preferred_element_type=jnp.float32).astype(
                jnp.bfloat16
            )
            results.append(
                lax.dot_general(
                    partial_value,
                    right_band,
                    (((1,), (1,)), ((), ())),
                    preferred_element_type=jnp.float32,
                )
            )
        return total + jnp.stack(results)

    start = jnp.zeros((nfreq, nstate, nstate), jnp.float32)
    left_all = lax.all_gather(left_pieces, "col", axis=0, tiled=True)

    def step(index, carry):
        left_band = lax.dynamic_index_in_dim(left_all, index, 0, False)
        return add_band(carry, left_band, index)

    total = lax.fori_loop(0, left_all.shape[0], step, start)
    summed = lax.psum(total, ("row", "col", "band"))
    owned = nstate // lax.axis_size(("row", "col", "band"))
    sigma = lax.dynamic_slice_in_dim(
        summed, lax.axis_index(("row", "col", "band")) * owned, owned, 1
    )
    return sigma


def solution(mesh):
    in_specs = (
        P(),
        P(),
        P("row", "col"),
        P("row", "col"),
        P(("col", "band"), None, "row"),
        P(("row", "band"), None, "col"),
    )
    out_specs = P(None, ("row", "col", "band"), None)
    return jax.shard_map(body, mesh=mesh, in_specs=in_specs, out_specs=out_specs, check_vma=False)
```

profile of v0, /device:TPU:0, one launch (start us, length us, event | category | flops | bytes accessed | tf_op | source)
XLA Modules:
  0.0 290.5 jit_solution(17561359348349133035)
XLA Ops:
  6.5 0.7 all-gather.3.cloned.1.call-update
  7.3 0.7 all-gather.5.cloned.1.call-update
  8.1 0.7 multiply_add_fusion
  8.7 48.6 %all-gather.3.cloned.1.call-done = bf16[4,256,1024]{2,1,0:T(8,128)(2,1)} async-done(((bf16[1,256,1024]{2,1,0:T(8,128)(2,1)}), bf16[4,256,1024]{2,1,0:T(8,128)(2,1)}) %all-gather.3.cloned.1.call-update) | async-done | bytes 2097168 | tf_op jit(solution)/shard_map/all_gather | solution.py:41
  57.3 35.9 %all-gather.5.cloned.1.call-done = bf16[4,256,1024]{2,1,0:T(8,128)(2,1)} async-done(((bf16[1,256,1024]{2,1,0:T(8,128)(2,1)}), bf16[4,256,1024]{2,1,0:T(8,128)(2,1)}) %all-gather.5.cloned.1.call-update) | async-done | bytes 2097168 | tf_op jit(solution)/shard_map/all_gather | solution.py:14
  93.2 59.5 %while.17 = (s32[]{:T(128)}, f32[2,256,256]{2,1,0:T(8,128)S(1)}, bf16[4,256,1024]{2,1,0:T(8,128)(2,1)}, f32[2]{0:T(128)S(1)}, s32[]{:T(128)}, /*index=5*/f32[8]{...) while((s32[]{:T(128)}, f32[2,256,256]{2,1,0:T(8,128)S(1)}, ...), condition=%wide.region_1.2_spmd.clone, body=%wide.region_0.1_spmd.clone.sunk | while | flops 1355677696 | bytes 20974844 | solution.py:47
  93.2 1.3 dynamic_slice.70
  94.5 0.6 fusion.34
  97.7 5.1 %convolution_bitcast_fusion.4 = f32[1,256,256]{2,1,0:T(8,128)S(1)} fusion(f32[1024,1024]{1,0:T(8,128)} %get-tuple-element.398, f32[1024,1024]{1,0:T(8,128)} %get-tuple-element.397, f32[]{:T(128)} %bitcast.32, bf16[4,256,1024]{2,1,0:T(8,128)(2,1)} %get-tuple-element.399, s32[]{:T(128)S(6)} %copy.9, bf16[4,256,1024]{2,1,0:T(8,128)(2,1)} %get-tuple-element.393), kind=kOutput, calls=%fused_computation.6.clone.1 | convolution fusion | flops 677642240 | bytes 9700864 | tf_op jit(solution)/shard_map/while/body/eval_jaxpr/dot_general | solution.py:31
  102.8 5.1 %convolution_bitcast_fusion.5 = f32[1,256,256]{2,1,0:T(8,128)S(1)} fusion(f32[1024,1024]{1,0:T(8,128)} %get-tuple-element.398, f32[1024,1024]{1,0:T(8,128)} %get-tuple-element.397, f32[]{:T(128)} %bitcast.33, bf16[4,256,1024]{2,1,0:T(8,128)(2,1)} %get-tuple-element.399, s32[]{:T(128)S(6)} %copy.9, bf16[4,256,1024]{2,1,0:T(8,128)(2,1)} %get-tuple-element.393), kind=kOutput, calls=%fused_computation.7.clone.1 | convolution fusion | flops 677642240 | bytes 9700864 | tf_op jit(solution)/shard_map/while/body/eval_jaxpr/dot_general | solution.py:31
  108.0 1.3 dynamic_slice.70
  109.4 0.6 fusion.34
  112.6 5.1 %convolution_bitcast_fusion.4 = f32[1,256,256]{2,1,0:T(8,128)S(1)} fusion(f32[1024,1024]{1,0:T(8,128)} %get-tuple-element.398, f32[1024,1024]{1,0:T(8,128)} %get-tuple-element.397, f32[]{:T(128)} %bitcast.32, bf16[4,256,1024]{2,1,0:T(8,128)(2,1)} %get-tuple-element.399, s32[]{:T(128)S(6)} %copy.9, bf16[4,256,1024]{2,1,0:T(8,128)(2,1)} %get-tuple-element.393), kind=kOutput, calls=%fused_computation.6.clone.1 | convolution fusion | flops 677642240 | bytes 9700864 | tf_op jit(solution)/shard_map/while/body/eval_jaxpr/dot_general | solution.py:31
  117.7 5.1 %convolution_bitcast_fusion.5 = f32[1,256,256]{2,1,0:T(8,128)S(1)} fusion(f32[1024,1024]{1,0:T(8,128)} %get-tuple-element.398, f32[1024,1024]{1,0:T(8,128)} %get-tuple-element.397, f32[]{:T(128)} %bitcast.33, bf16[4,256,1024]{2,1,0:T(8,128)(2,1)} %get-tuple-element.399, s32[]{:T(128)S(6)} %copy.9, bf16[4,256,1024]{2,1,0:T(8,128)(2,1)} %get-tuple-element.393), kind=kOutput, calls=%fused_computation.7.clone.1 | convolution fusion | flops 677642240 | bytes 9700864 | tf_op jit(solution)/shard_map/while/body/eval_jaxpr/dot_general | solution.py:31
  122.9 1.3 dynamic_slice.70
  124.2 0.6 fusion.34
  127.5 5.1 %convolution_bitcast_fusion.4 = f32[1,256,256]{2,1,0:T(8,128)S(1)} fusion(f32[1024,1024]{1,0:T(8,128)} %get-tuple-element.398, f32[1024,1024]{1,0:T(8,128)} %get-tuple-element.397, f32[]{:T(128)} %bitcast.32, bf16[4,256,1024]{2,1,0:T(8,128)(2,1)} %get-tuple-element.399, s32[]{:T(128)S(6)} %copy.9, bf16[4,256,1024]{2,1,0:T(8,128)(2,1)} %get-tuple-element.393), kind=kOutput, calls=%fused_computation.6.clone.1 | convolution fusion | flops 677642240 | bytes 9700864 | tf_op jit(solution)/shard_map/while/body/eval_jaxpr/dot_general | solution.py:31
  132.5 5.1 %convolution_bitcast_fusion.5 = f32[1,256,256]{2,1,0:T(8,128)S(1)} fusion(f32[1024,1024]{1,0:T(8,128)} %get-tuple-element.398, f32[1024,1024]{1,0:T(8,128)} %get-tuple-element.397, f32[]{:T(128)} %bitcast.33, bf16[4,256,1024]{2,1,0:T(8,128)(2,1)} %get-tuple-element.399, s32[]{:T(128)S(6)} %copy.9, bf16[4,256,1024]{2,1,0:T(8,128)(2,1)} %get-tuple-element.393), kind=kOutput, calls=%fused_computation.7.clone.1 | convolution fusion | flops 677642240 | bytes 9700864 | tf_op jit(solution)/shard_map/while/body/eval_jaxpr/dot_general | solution.py:31
  137.8 1.3 dynamic_slice.70
  142.3 5.1 %convolution_bitcast_fusion.4 = f32[1,256,256]{2,1,0:T(8,128)S(1)} fusion(f32[1024,1024]{1,0:T(8,128)} %get-tuple-element.398, f32[1024,1024]{1,0:T(8,128)} %get-tuple-element.397, f32[]{:T(128)} %bitcast.32, bf16[4,256,1024]{2,1,0:T(8,128)(2,1)} %get-tuple-element.399, s32[]{:T(128)S(6)} %copy.9, bf16[4,256,1024]{2,1,0:T(8,128)(2,1)} %get-tuple-element.393), kind=kOutput, calls=%fused_computation.6.clone.1 | convolution fusion | flops 677642240 | bytes 9700864 | tf_op jit(solution)/shard_map/while/body/eval_jaxpr/dot_general | solution.py:31
  147.4 5.1 %convolution_bitcast_fusion.5 = f32[1,256,256]{2,1,0:T(8,128)S(1)} fusion(f32[1024,1024]{1,0:T(8,128)} %get-tuple-element.398, f32[1024,1024]{1,0:T(8,128)} %get-tuple-element.397, f32[]{:T(128)} %bitcast.33, bf16[4,256,1024]{2,1,0:T(8,128)(2,1)} %get-tuple-element.399, s32[]{:T(128)S(6)} %copy.9, bf16[4,256,1024]{2,1,0:T(8,128)(2,1)} %get-tuple-element.393), kind=kOutput, calls=%fused_computation.7.clone.1 | convolution fusion | flops 677642240 | bytes 9700864 | tf_op jit(solution)/shard_map/while/body/eval_jaxpr/dot_general | solution.py:31
  152.6 0.8 copy-done
  153.4 129.2 %all-reduce.2.cloned.1.call-done = f32[2,256,256]{2,1,0:T(8,128)} async-done(((f32[2,256,256]{2,1,0:T(8,128)}), f32[2,256,256]{2,1,0:T(8,128)}) %all-reduce.2.cloned.1.call-update) | async-done | bytes 524304 | tf_op jit(solution)/shard_map/psum | solution.py:48
  282.6 1.3 constant_dynamic-slice_fusion
  (11 shorter events, 1.3 us)
Async XLA Ops:
  6.5 50.8 %all-gather.3.cloned.1.call-start = ((), (), s32[]{:S(2)}) async-start(), calls=%async_computation | async-start | bytes 2621440 | tf_op jit(solution)/shard_map/all_gather | solution.py:41
  7.3 85.9 %all-gather.5.cloned.1.call-start = ((), (), s32[]{:S(2)}) async-start(), calls=%async_computation.1 | async-start | bytes 2621440 | tf_op jit(solution)/shard_map/all_gather | solution.py:14
  8.0 274.6 %all-reduce.2.cloned.1.call-start = ((), (), s32[]{:S(2)}) async-start(), calls=%async_computation.2 | async-start | bytes 1048576 | tf_op jit(solution)/shard_map/psum | solution.py:48
  152.6 0.8 copy-start
Sparse Core Ops, SparseCore 0:
  8.9 48.3 all-gather.2
  59.2 33.9 all-gather.4
  153.6 129.0 all-reduce.1
where the time goes:
time: 291 us; the launch traced here: 290 us
  waiting for transfers between devices  215 us (74%)
  matrix products  40.5 us (14%)
  between operations  13.1 us (5%)
  loops' own time  10.7 us (4%)
  local copies, waits for them, and re-layouts  9.74 us (3%)
    psum x1, waiting for transfers between devices, body(): summed = lax.psum(total, ('row', 'col', 'band'))  129 us
    all_gather x1, waiting for transfers between devices, body(): left_all = lax.all_gather(left_pieces, 'col', axis=0, tiled=True)  48.6 us
    dot_general x8, matrix products, add_band(): lax.dot_general(partial_value, right_band, (((1,), (1,)), ((), ())), pref...  40.5 us
    all_gather x1, waiting for transfers between devices, body(): right_all = lax.all_gather(right_pieces, 'row', axis=0, tiled=True)  35.9 us
    another operation x1, loops' own time, body(): total = lax.fori_loop(0, left_all.shape[0], step, start)  10.7 us
  transfers between devices with their start and end apart: 3, of which 3 were waited for; matrix products, arithmetic and copies ran while one was open for 0% of the time, Pallas kernels for 0%

commit v1 on v0

--- a/solution.py
+++ b/solution.py
@@ -38,7 +38,12 @@
         return total + jnp.stack(results)
 
     start = jnp.zeros((nfreq, nstate, nstate), jnp.float32)
-    left_all = lax.all_gather(left_pieces, "col", axis=0, tiled=True)
+    ring = [left_pieces]
+    for hop in range(3):
+        ring.append(lax.ppermute(ring[-1], "col", [(dev, (dev + 1) % 4) for dev in range(4)]))
+    left_all = jnp.roll(
+        jnp.concatenate(ring[::-1], axis=0), (lax.axis_index("col") + 1) * ring[0].shape[0], axis=0
+    )
 
     def step(index, carry):
         left_band = lax.dynamic_index_in_dim(left_all, index, 0, False)

time: 291 us -> 246 us (0.85)
  waiting for transfers between devices: 215 us -> 170 us
  starting transfers between devices: 0.08 us -> 3.15 us
    all_gather x1 -> x0, waiting for transfers between devices: 48.6 us -> none  [body(): left_all = lax.all_gather(left_pieces, 'col', axis=0, tiled=True)]
    ppermute x0 -> x3, waiting for transfers between devices: none -> 42.4 us  [body(): lax.ppermute(ring[-1], 'col', [(dev, (dev + 1) % 4) for dev in range(4)])]
    all_gather x1, waiting for transfers between devices: 35.9 us -> 0.02 us  [body(): right_all = lax.all_gather(right_pieces, 'row', axis=0, tiled=True)]
    ppermute x0 -> x3, starting transfers between devices: none -> 3.11 us  [body(): lax.ppermute(ring[-1], 'col', [(dev, (dev + 1) % 4) for dev in range(4)])]
  transfers between devices with their start and end apart: 3 -> 5, of which waited for: 3 -> 4; matrix products, arithmetic and copies ran while one was open for 0% -> 1% of each run, Pallas kernels for 0% -> 0%
where the time goes in v1:
time: 246 us
  waiting for transfers between devices  170 us (69%)
  matrix products  39.4 us (16%)
  between operations  13.5 us (5%)
  loops' own time  9.88 us (4%)
  local copies, waits for them, and re-layouts  8.5 us (3%)
  starting transfers between devices  3.15 us (1%)
    psum x1, waiting for transfers between devices, body(): summed = lax.psum(total, ('row', 'col', 'band'))  127 us
    ppermute x3, waiting for transfers between devices, body(): lax.ppermute(ring[-1], 'col', [(dev, (dev + 1) % 4) for dev in range(4)])  42.4 us
    dot_general x8, matrix products, add_band(): lax.dot_general(partial_value, right_band, (((1,), (1,)), ((), ())), pref...  39.4 us
    another operation x1, loops' own time, body(): total = lax.fori_loop(0, left_all.shape[0], step, start)  9.88 us
  transfers between devices with their start and end apart: 5, of which 4 were waited for; matrix products, arithmetic and copies ran while one was open for 1% of the time, Pallas kernels for 0%

profile of v1, /device:TPU:0, one launch (start us, length us, event | category | flops | bytes accessed | tf_op | source)
XLA Modules:
  0.0 245.9 jit_solution(14621946874608073002)
XLA Ops:
  6.5 0.7 all-gather.2.cloned.1.call-update
  7.3 3.1 %collective-permute-start = (bf16[1,256,1024]{2,1,0:T(8,128)(2,1)}, bf16[1,256,1024]{2,1,0:T(8,128)(2,1)S(1)}, u32[]{:S(2)}, u32[]{:S(2)}) collective-permute-start(bf16[1,256,1024]{2,1,0:T(8,128)(2,1)} %param.12), channel_id=1, source_target_pairs={{0,2},{2,4},{4,6},{6,0},{1,3},{3,5},{5,7},{7,1},{8,10},{10,12},{12... | collective-permute-start | bytes 1572872 | tf_op jit(solution)/shard_map/ppermute | solution.py:43
  10.4 14.2 %collective-permute-done = bf16[1,256,1024]{2,1,0:T(8,128)(2,1)S(1)} collective-permute-done((bf16[1,256,1024]{2,1,0:T(8,128)(2,1)}, bf16[1,256,1024]{2,1,0:T(8,128)(2,1)S(1)}, u32[]{:S(2)}, u32[]{:S(2)}) %collective-permute-start) | collective-permute-done | bytes 524320 | tf_op jit(solution)/shard_map/ppermute | solution.py:43
  24.6 14.9 %collective-permute-done.1 = bf16[1,256,1024]{2,1,0:T(8,128)(2,1)S(1)} collective-permute-done((bf16[1,256,1024]{2,1,0:T(8,128)(2,1)S(1)}, bf16[1,256,1024]{2,1,0:T(8,128)(2,1)S(1)}, u32[]{:S(2)}, u32[]{:S(2)}) %collective-permute-start.1) | collective-permute-done | bytes 524320 | tf_op jit(solution)/shard_map/ppermute | solution.py:43
  39.5 0.7 multiply_add_fusion
  40.1 13.4 %collective-permute-done.2 = bf16[1,256,1024]{2,1,0:T(8,128)(2,1)S(1)} collective-permute-done((bf16[1,256,1024]{2,1,0:T(8,128)(2,1)S(1)}, bf16[1,256,1024]{2,1,0:T(8,128)(2,1)S(1)}, u32[]{:S(2)}, u32[]{:S(2)}) %collective-permute-start.2) | collective-permute-done | bytes 524320 | tf_op jit(solution)/shard_map/ppermute | solution.py:43
  53.6 1.1 constant_dynamic-update-slice_fusion.4
  55.4 54.5 %while.17 = (s32[]{:T(128)}, f32[2,256,256]{2,1,0:T(8,128)S(1)}, bf16[4,256,1024]{2,1,0:T(8,128)(2,1)S(1)}, f32[2]{0:T(128)S(1)}, s32[]{:T(128)}, /*index=5*/f32...) while((s32[]{:T(128)}, f32[2,256,256]{2,1,0:T(8,128)S(1)}, ...), condition=%wide.region_1.2_spmd.clone, body=%wide.region_0.1_spmd.clone.sunk | while | flops 1355677696 | bytes 20974836 | solution.py:52
  55.4 0.6 dynamic_slice.76
  56.0 0.6 fusion.34
  57.8 4.9 %convolution_bitcast_fusion.5 = f32[1,256,256]{2,1,0:T(8,128)S(1)} fusion(f32[1024,1024]{1,0:T(8,128)} %get-tuple-element.398, f32[1024,1024]{1,0:T(8,128)} %get-tuple-element.397, f32[]{:T(128)} %bitcast.33, bf16[4,256,1024]{2,1,0:T(8,128)(2,1)} %get-tuple-element.399, s32[]{:T(128)} %get-tuple-element.378, ...), kind=kOutput, calls=%fused_computation.7.clone.1 | convolution fusion | flops 677642240 | bytes 9700864 | tf_op jit(solution)/shard_map/while/body/eval_jaxpr/dot_general | solution.py:31
  63.9 4.9 %convolution_bitcast_fusion.4 = f32[1,256,256]{2,1,0:T(8,128)S(1)} fusion(f32[1024,1024]{1,0:T(8,128)} %get-tuple-element.398, f32[1024,1024]{1,0:T(8,128)} %get-tuple-element.397, f32[]{:T(128)} %bitcast.32, bf16[4,256,1024]{2,1,0:T(8,128)(2,1)} %get-tuple-element.399, s32[]{:T(128)} %get-tuple-element.378, ...), kind=kOutput, calls=%fused_computation.6.clone.1 | convolution fusion | flops 677642240 | bytes 9700864 | tf_op jit(solution)/shard_map/while/body/eval_jaxpr/dot_general | solution.py:31
  69.0 0.6 dynamic_slice.76
  71.4 4.9 %convolution_bitcast_fusion.5 = f32[1,256,256]{2,1,0:T(8,128)S(1)} fusion(f32[1024,1024]{1,0:T(8,128)} %get-tuple-element.398, f32[1024,1024]{1,0:T(8,128)} %get-tuple-element.397, f32[]{:T(128)} %bitcast.33, bf16[4,256,1024]{2,1,0:T(8,128)(2,1)} %get-tuple-element.399, s32[]{:T(128)} %get-tuple-element.378, ...), kind=kOutput, calls=%fused_computation.7.clone.1 | convolution fusion | flops 677642240 | bytes 9700864 | tf_op jit(solution)/shard_map/while/body/eval_jaxpr/dot_general | solution.py:31
  77.5 4.9 %convolution_bitcast_fusion.4 = f32[1,256,256]{2,1,0:T(8,128)S(1)} fusion(f32[1024,1024]{1,0:T(8,128)} %get-tuple-element.398, f32[1024,1024]{1,0:T(8,128)} %get-tuple-element.397, f32[]{:T(128)} %bitcast.32, bf16[4,256,1024]{2,1,0:T(8,128)(2,1)} %get-tuple-element.399, s32[]{:T(128)} %get-tuple-element.378, ...), kind=kOutput, calls=%fused_computation.6.clone.1 | convolution fusion | flops 677642240 | bytes 9700864 | tf_op jit(solution)/shard_map/while/body/eval_jaxpr/dot_general | solution.py:31
  82.6 0.6 dynamic_slice.76
  85.0 4.9 %convolution_bitcast_fusion.5 = f32[1,256,256]{2,1,0:T(8,128)S(1)} fusion(f32[1024,1024]{1,0:T(8,128)} %get-tuple-element.398, f32[1024,1024]{1,0:T(8,128)} %get-tuple-element.397, f32[]{:T(128)} %bitcast.33, bf16[4,256,1024]{2,1,0:T(8,128)(2,1)} %get-tuple-element.399, s32[]{:T(128)} %get-tuple-element.378, ...), kind=kOutput, calls=%fused_computation.7.clone.1 | convolution fusion | flops 677642240 | bytes 9700864 | tf_op jit(solution)/shard_map/while/body/eval_jaxpr/dot_general | solution.py:31
  91.2 4.9 %convolution_bitcast_fusion.4 = f32[1,256,256]{2,1,0:T(8,128)S(1)} fusion(f32[1024,1024]{1,0:T(8,128)} %get-tuple-element.398, f32[1024,1024]{1,0:T(8,128)} %get-tuple-element.397, f32[]{:T(128)} %bitcast.32, bf16[4,256,1024]{2,1,0:T(8,128)(2,1)} %get-tuple-element.399, s32[]{:T(128)} %get-tuple-element.378, ...), kind=kOutput, calls=%fused_computation.6.clone.1 | convolution fusion | flops 677642240 | bytes 9700864 | tf_op jit(solution)/shard_map/while/body/eval_jaxpr/dot_general | solution.py:31
  96.3 0.6 dynamic_slice.76
  98.7 4.9 %convolution_bitcast_fusion.5 = f32[1,256,256]{2,1,0:T(8,128)S(1)} fusion(f32[1024,1024]{1,0:T(8,128)} %get-tuple-element.398, f32[1024,1024]{1,0:T(8,128)} %get-tuple-element.397, f32[]{:T(128)} %bitcast.33, bf16[4,256,1024]{2,1,0:T(8,128)(2,1)} %get-tuple-element.399, s32[]{:T(128)} %get-tuple-element.378, ...), kind=kOutput, calls=%fused_computation.7.clone.1 | convolution fusion | flops 677642240 | bytes 9700864 | tf_op jit(solution)/shard_map/while/body/eval_jaxpr/dot_general | solution.py:31
  104.8 4.9 %convolution_bitcast_fusion.4 = f32[1,256,256]{2,1,0:T(8,128)S(1)} fusion(f32[1024,1024]{1,0:T(8,128)} %get-tuple-element.398, f32[1024,1024]{1,0:T(8,128)} %get-tuple-element.397, f32[]{:T(128)} %bitcast.32, bf16[4,256,1024]{2,1,0:T(8,128)(2,1)} %get-tuple-element.399, s32[]{:T(128)} %get-tuple-element.378, ...), kind=kOutput, calls=%fused_computation.6.clone.1 | convolution fusion | flops 677642240 | bytes 9700864 | tf_op jit(solution)/shard_map/while/body/eval_jaxpr/dot_general | solution.py:31
  109.9 0.8 copy-done
  110.7 127.0 %all-reduce.2.cloned.1.call-done = f32[2,256,256]{2,1,0:T(8,128)} async-done(((f32[2,256,256]{2,1,0:T(8,128)}), f32[2,256,256]{2,1,0:T(8,128)}) %all-reduce.2.cloned.1.call-update) | async-done | bytes 524304 | tf_op jit(solution)/shard_map/psum | solution.py:53
  237.7 1.3 constant_dynamic-slice_fusion
  (27 shorter events, 3.0 us)
Async XLA Ops:
  6.5 48.3 %copy-start.1 = (bf16[1,256,1024]{2,1,0:T(8,128)(2,1)S(1)}, bf16[1,256,1024]{2,1,0:T(8,128)(2,1)}, u32[]{:S(2)}) copy-start(bf16[1,256,1024]{2,1,0:T(8,128)(2,1)} %param.12) | copy-start | bytes 1572868
  6.5 48.6 %all-gather.2.cloned.1.call-start = ((), (), s32[]{:S(2)}) async-start(), calls=%async_computation | async-start | bytes 2621440 | tf_op jit(solution)/shard_map/all_gather | solution.py:14
  7.3 230.5 %all-reduce.2.cloned.1.call-start = ((), (), s32[]{:S(2)}) async-start(), calls=%async_computation.1 | async-start | bytes 1048576 | tf_op jit(solution)/shard_map/psum | solution.py:53
  7.3 17.3 %collective-permute-start = (bf16[1,256,1024]{2,1,0:T(8,128)(2,1)}, bf16[1,256,1024]{2,1,0:T(8,128)(2,1)S(1)}, u32[]{:S(2)}, u32[]{:S(2)}) collective-permute-start(bf16[1,256,1024]{2,1,0:T(8,128)(2,1)} %param.12), channel_id=1, source_target_pairs={{0,2},{2,4},{4,6},{6,0},{1,3},{3,5},{5,7},{7,1},{8,10},{10,12},{12... | collective-permute-start | bytes 1572872 | tf_op jit(solution)/shard_map/ppermute | solution.py:43
  24.6 14.9 %collective-permute-start.1 = (bf16[1,256,1024]{2,1,0:T(8,128)(2,1)S(1)}, bf16[1,256,1024]{2,1,0:T(8,128)(2,1)S(1)}, u32[]{:S(2)}, u32[]{:S(2)}) collective-permute-start(bf16[1,256,1024]{2,1,0:T(8,128)(2,1)S(1)} %collective-permute-done), channel_id=1, source_target_pairs={{0,2},{2,4},{4,6},{6,0},{1,3},{3,5},{5,7},{7,1},{8,10},{10,12},{12... | collective-permute-start | bytes 1572872 | tf_op jit(solution)/shard_map/ppermute | solution.py:43
  39.5 14.0 %collective-permute-start.2 = (bf16[1,256,1024]{2,1,0:T(8,128)(2,1)S(1)}, bf16[1,256,1024]{2,1,0:T(8,128)(2,1)S(1)}, u32[]{:S(2)}, u32[]{:S(2)}) collective-permute-start(bf16[1,256,1024]{2,1,0:T(8,128)(2,1)S(1)} %collective-permute-done.1), channel_id=1, source_target_pairs={{0,2},{2,4},{4,6},{6,0},{1,3},{3,5},{5,7},{7,1},{8,10},{10,12},{12... | collective-permute-start | bytes 1572872 | tf_op jit(solution)/shard_map/ppermute | solution.py:43
  54.7 0.7 copy-start.2
  109.9 0.8 copy-start
Sparse Core Ops, SparseCore 0:
  9.2 37.8 all-gather.1
  110.8 126.8 all-reduce.1
